TPU v7x, 32 devices: a whole 2x2x4 slice. The times are simulated.
32 devices in a mesh: dom: 32 (over z, y, x, core).
Axes of the slice: x: 2, y: 2, z: 4, core: 2. Of those that a mesh axis runs over, the one named last changes fastest.
Arguments:
- right_side: float32 [18, 32768], P(None, 'dom'), may hold values from -20 to 20
- element_matrix: bfloat16 [72, 72, 16384], P(None, None, 'dom'), may hold values from -8 to 8, as said below
- face_map: int32 [4, 16384], P(None, 'dom'), may hold values from 0 to 1535
- share_index: int32 [32, 4, 128], P('dom'), may hold values from 0 to 1023
- share_count: int32 [32, 4], P('dom'), may hold values from 0 to 128, as said below
- face_mass: float32 [32768], P('dom'), may hold values from 0.5 to 2
- absorbing: int32 [32768], P('dom'), may hold values 0 or 1
- impedance: float32 [32768], P('dom'), may hold values from 0.5 to 4
Outputs:
- solution: float32 [18, 32768], P(None, 'dom')
- residual: float32 [18, 32768], P(None, 'dom')
Inputs may be any that keep to these rules, and one draw needn't show every extreme that they name: `element_matrix`: each element's 72 x 72 matrix is symmetric positive definite. share_count[d, k] is 0 where device d + o_k lies outside the axis; it equals 128 for some device and offset in every draw.
All inputs are finite; a program needn't handle non-finite values. No bound on the sum of `absorbing` on one device may be relied on, other than what follows from the above.
Results may differ from a plain program's by a relative error of at most 0.0003.
Values sent between devices are 32-bit elements; how exact they have to be, the bound alone decides.
A program may use at most 64 MiB of HBM per device.

v0:
```python
import functools
import jax
import jax.numpy as jnp
from jax import lax
from jax.experimental import pallas as pl
from jax.experimental.pallas import tpu as pltpu
from jax.sharding import PartitionSpec as P

LANES = 128
WIDE = 256
MESH = pl.DeviceIdType.MESH
F32 = jnp.float32
BF16 = jnp.bfloat16


def offset_list(block_count):
    half_count = block_count // 2
    return [
        block_index - half_count if block_index < half_count else block_index - half_count + 1
        for block_index in range(block_count)
    ]


def split3(x):
    high = x.astype(BF16)
    rest = x - high.astype(F32)
    middle = rest.astype(BF16)
    low = (rest - middle.astype(F32)).astype(BF16)
    return jnp.concatenate([high, middle, low], axis=0)


def sum3(x):
    rows = x.shape[0] // 3
    return x[:rows] + (x[rows : 2 * rows] + x[2 * rows :])


def dot(a, b):
    return lax.dot_general(a, b, (((1,), (0,)), ((), ())), preferred_element_type=F32)


def dot_nt(a, b):
    return lax.dot_general(a, b, (((1,), (1,)), ((), ())), preferred_element_type=F32)


def kernel(
    cfg,
    rs_in, em_ref, fm_in, si_in, sc_in, mass_in, absorb_in, imp_in,
    sol_ref, res_ref,
    rs_ref, fm_ref, si_ref, sc_ref, mass_ref, absorb_ref, imp_ref,
    em_buf, pick_map, send_map, out_buf, ghost_buf, part_buf, ret_buf,
    picked, prod, spread_own, spread_ghost, b_buf, q_buf, sum1, sum2, sum_all,
    in_sem, em_sem, fetch_send, fetch_recv, ret_send, ret_recv,
    s1_send, s1_recv, s2_send, s2_recv, all_send, all_recv,
):
    n, g1, g2, trace, sides, elements, own, blocks, width = cfg
    offsets = offset_list(blocks)
    pad = -(-trace // 8) * 8
    own_hi = own // WIDE
    ghost_hi = blocks * width // WIDE
    chunks = sides * elements // WIDE
    per_side = elements // WIDE
    rows_own, rows_ghost = own_hi * pad, ghost_hi * pad
    me = lax.axis_index("dom")
    block_of, in_block = me // g1, lax.rem(me, g1)

    barrier = pltpu.get_barrier_semaphore()
    waits = jnp.int32((g1 - 1) + (g2 - 1))
    for o in offsets:
        there = me + o
        inside = (there >= 0) & (there < n)
        waits = waits + inside.astype(jnp.int32)

        @pl.when(inside)
        def _():
            pl.semaphore_signal(barrier, inc=1, device_id=(there,), device_id_type=MESH)

    def peer1(d):
        return block_of * g1 + lax.rem(in_block + d, g1)

    def peer2(d):
        return lax.rem(block_of + d, g2) * g1 + in_block

    for d in range(1, g1):
        pl.semaphore_signal(barrier, inc=1, device_id=(peer1(d),), device_id_type=MESH)
    for d in range(1, g2):
        pl.semaphore_signal(barrier, inc=1, device_id=(peer2(d),), device_id_type=MESH)

    in_copies = [
        pltpu.make_async_copy(source, target, in_sem.at[i])
        for i, (source, target) in enumerate(
            (
                (rs_in, rs_ref), (si_in, si_ref), (sc_in, sc_ref), (fm_in, fm_ref),
                (mass_in, mass_ref), (absorb_in, absorb_ref), (imp_in, imp_ref),
            )
        )
    ]
    for copy in in_copies:
        copy.start()
    em_copies = [
        pltpu.make_async_copy(
            em_ref.at[pl.ds(s * trace, trace)], em_buf.at[pl.ds(s * trace, trace)], em_sem.at[s]
        )
        for s in range(sides)
    ]
    for copy in em_copies:
        copy.start()

    for copy in in_copies[:3]:
        copy.wait()
    lo_iota = lax.broadcasted_iota(jnp.int32, (WIDE, WIDE), 0)
    slot_iota = lax.broadcasted_iota(jnp.int32, (1, width), 1)
    per_wide = WIDE // width
    send_hi = []
    for h in range(ghost_hi):
        cols = []
        for k in range(h * per_wide, (h + 1) * per_wide):
            alive = slot_iota < sc_ref[0:1, k : k + 1]
            cols.append(jnp.where(alive, si_ref[0, k : k + 1, :], -1))
        index = jnp.concatenate(cols, axis=1)
        low = jnp.where(index < 0, -1, index & (WIDE - 1))
        send_map[:, h * WIDE : (h + 1) * WIDE] = (lo_iota == low).astype(F32).astype(BF16)
        send_hi.append(index >> 8)

    def pick_hi(index, stacked, count):
        value = jnp.zeros((pad, WIDE), F32)
        for h in range(count):
            value = jnp.where(index == h, stacked[h * pad : (h + 1) * pad], value)
        return value

    def send_of(split, rnd):
        for h in range(ghost_hi):
            got = sum3(dot(split, send_map[:, h * WIDE : (h + 1) * WIDE]))
            out_buf[rnd, h * pad : (h + 1) * pad, :] = pick_hi(send_hi[h], got, own_hi)

    def piece(ref, rnd, k):
        h, lane = k // per_wide, (k % per_wide) * width
        return ref.at[rnd, pl.ds(h * pad, pad), pl.ds(lane, width)]

    def halo(src, dst, send_sem, recv_sem, rnd, k, step):
        there = me + step
        copy = pltpu.make_async_remote_copy(
            src_ref=piece(src, rnd, k), dst_ref=piece(dst, rnd, k),
            send_sem=send_sem.at[rnd, k], recv_sem=recv_sem.at[rnd, k],
            device_id=(there,), device_id_type=MESH,
        )
        came = me - step
        return copy, (there >= 0) & (there < n), (came >= 0) & (came < n)

    def fetch(rnd, k):
        return halo(out_buf, ghost_buf, fetch_send, fetch_recv, rnd, k, offsets[k])

    def giveback(rnd, k):
        return halo(part_buf, ret_buf, ret_send, ret_recv, rnd, k, -offsets[k])

    far_first = sorted(range(blocks), key=lambda k: -abs(offsets[k]))

    def start_all(make, rnd):
        for k in far_first:
            copy, to, _ = make(rnd, k)
            pl.when(to)(copy.start)

    def wait_recv_all(make, rnd):
        for k in range(blocks):
            copy, _, came = make(rnd, k)
            pl.when(came)(copy.wait_recv)

    def wait_send_all(make, rnd):
        for k in range(blocks):
            copy, to, _ = make(rnd, k)
            pl.when(to)(copy.wait_send)

    b_buf[...] = jnp.zeros_like(b_buf)
    for h in range(own_hi):
        b_buf[h * pad : h * pad + trace, :] = rs_ref[:, h * WIDE : (h + 1) * WIDE]
    b_split = split3(b_buf[...])
    send_of(b_split, 0)
    for k in range(blocks):
        for rnd in range(2):
            for ref, step in ((ghost_buf, offsets[k]), (ret_buf, -offsets[k])):
                came = me - step

                @pl.when((came < 0) | (came >= n))
                def _():
                    h, lane = k // per_wide, (k % per_wide) * width
                    ref[rnd, h * pad : (h + 1) * pad, lane : lane + width] = jnp.zeros(
                        (pad, width), F32
                    )

    pl.semaphore_wait(barrier, waits)
    start_all(fetch, 0)

    for copy in in_copies[3:]:
        copy.wait()
    hi_of = []
    for c in range(chunks):
        s, lane = c // per_side, (c % per_side) * WIDE
        index = fm_ref[s : s + 1, lane : lane + WIDE]
        low = index & (WIDE - 1)
        pick_map[:, c * WIDE : (c + 1) * WIDE] = (lo_iota == low).astype(F32).astype(BF16)
        hi_of.append(index >> 8)
    prod[...] = jnp.zeros_like(prod)
    row_live = lax.broadcasted_iota(jnp.int32, (pad, WIDE), 0) < trace
    diag_row = mass_ref[...] + absorb_ref[...].astype(F32) * imp_ref[...]

    def diagonal_times(x):
        return jnp.concatenate(
            [
                x[h * pad : (h + 1) * pad] * diag_row[:, h * WIDE : (h + 1) * WIDE]
                for h in range(own_hi)
            ],
            axis=0,
        )

    def operate(x, split, rnd, after_product):
        for c in range(chunks):
            s, lane = c // per_side, (c % per_side) * WIDE
            got = sum3(dot(split, pick_map[:, c * WIDE : (c + 1) * WIDE]))
            picked[s, :, lane : lane + WIDE] = pick_hi(hi_of[c], got, own_hi)
        wait_recv_all(fetch, rnd)
        ghost_split = split3(ghost_buf[rnd])
        for c in range(chunks):
            s, lane = c // per_side, (c % per_side) * WIDE
            got = sum3(dot(ghost_split, pick_map[:, c * WIDE : (c + 1) * WIDE]))
            picked[s, :, lane : lane + WIDE] += pick_hi(hi_of[c] - own_hi, got, ghost_hi)
        if rnd == 0:
            for copy in em_copies:
                copy.wait()
        for t in range(elements // LANES):
            lanes = slice(t * LANES, (t + 1) * LANES)

            def body(s, acc):
                for c in range(trace):
                    row = picked[s, c : c + 1, lanes]
                    acc = acc + em_buf[s * trace + c, :, lanes].astype(F32) * row
                return acc

            prod[0 : sides * trace, lanes] = lax.fori_loop(
                0, sides, body, jnp.zeros((sides * trace, LANES), F32)
            )

        def spread(c):
            s, lane = c // per_side, (c % per_side) * WIDE
            value = prod[s * trace : s * trace + pad, lane : lane + WIDE]
            return jnp.where(row_live, value, 0.0)

        after_product()
        for c in range(chunks):
            value = spread(c)
            stacked = jnp.concatenate(
                [jnp.where(hi_of[c] == own_hi + h, value, 0.0) for h in range(ghost_hi)], axis=0
            )
            spread_ghost[:, c * WIDE : (c + 1) * WIDE] = split3(stacked)
        part_buf[rnd] = sum3(dot_nt(spread_ghost[...], pick_map[...]))
        start_all(giveback, rnd)
        for c in range(chunks):
            value = spread(c)
            stacked = jnp.concatenate(
                [jnp.where(hi_of[c] == h, value, 0.0) for h in range(own_hi)], axis=0
            )
            spread_own[:, c * WIDE : (c + 1) * WIDE] = split3(stacked)
        result = sum3(dot_nt(spread_own[...], pick_map[...])) + diagonal_times(x)
        wait_recv_all(giveback, rnd)
        came_back = []
        for h in range(ghost_hi):
            value = ret_buf[rnd, h * pad : (h + 1) * pad, :]
            stacked = jnp.concatenate(
                [jnp.where(send_hi[h] == i, value, 0.0) for i in range(own_hi)], axis=0
            )
            came_back.append(split3(stacked))
        result = result + sum3(dot_nt(jnp.concatenate(came_back, axis=1), send_map[...]))
        return result

    def stage1(d):
        slot = sum1.at[in_block]
        return pltpu.make_async_remote_copy(
            src_ref=slot, dst_ref=slot, send_sem=s1_send.at[d], recv_sem=s1_recv.at[d],
            device_id=(peer1(d),), device_id_type=MESH,
        )

    def stage2(d):
        slot = sum2.at[block_of]
        return pltpu.make_async_remote_copy(
            src_ref=slot, dst_ref=slot, send_sem=s2_send.at[d], recv_sem=s2_recv.at[d],
            device_id=(peer2(d),), device_id_type=MESH,
        )

    def lane_sums(x):
        total = jnp.sum(x, axis=0, keepdims=True)
        return total[:, :LANES] + total[:, LANES:]

    def pair_of(x, y):
        return jnp.concatenate([lane_sums(x), lane_sums(y)], axis=0)

    def begin_sum(x, y):
        sum1[in_block] = pair_of(x, y)
        for d in range(1, g1):
            stage1(d).start()

    def middle_sum():
        for d in range(1, g1):
            stage1(d).wait_recv()
        sum2[block_of] = jnp.sum(sum1[...], axis=0)
        for d in range(1, g2):
            stage2(d).start()

    def totals(parts):
        total = jnp.sum(jnp.sum(parts, axis=0), axis=1, keepdims=True)
        return total[0:1], total[1:2]

    def end_sum():
        for d in range(1, g2):
            stage2(d).wait_recv()
        return totals(sum2[...])

    def straight(d):
        return pltpu.make_async_remote_copy(
            src_ref=sum_all.at[0], dst_ref=sum_all.at[d],
            send_sem=all_send.at[d], recv_sem=all_recv.at[d],
            device_id=(lax.rem(me + d, n),), device_id_type=MESH,
        )

    def sum_straight(x, y):
        sum_all[0] = pair_of(x, y)
        for d in sorted(range(1, n), key=lambda d: abs(2 * d - n)):
            straight(d).start()
        for d in range(1, n):
            straight(d).wait_recv()
        return totals(sum_all[...])

    q = operate(b_buf[...], b_split, 0, lambda: None)
    q_buf[...] = q
    q_split = split3(q)
    send_of(q_split, 1)
    start_all(fetch, 1)
    b = b_buf[...]
    begin_sum(b * b, b * q)
    w = operate(q_buf[...], q_split, 1, middle_sum)
    rr, curve = end_sum()
    step0 = rr / curve
    b, q = b_buf[...], q_buf[...]
    r1 = b - step0 * q
    z1 = q - step0 * w
    new, curve = sum_straight(r1 * r1, r1 * z1)
    beta = new / rr
    step1 = new / (curve - beta * new / step0)
    sol = step0 * b + step1 * (r1 + beta * b)
    res = r1 - step1 * (z1 + beta * q)
    for h in range(own_hi):
        sol_ref[:, h * WIDE : (h + 1) * WIDE] = sol[h * pad : h * pad + trace]
        res_ref[:, h * WIDE : (h + 1) * WIDE] = res[h * pad : h * pad + trace]
    for rnd in range(2):
        wait_send_all(fetch, rnd)
        wait_send_all(giveback, rnd)
    for d in range(1, g1):
        stage1(d).wait_send()
    for d in range(1, g2):
        stage2(d).wait_send()
    for d in range(1, n):
        straight(d).wait_send()


def put_out(sol_ref, res_ref, sol_out, res_out, sems):
    copies = [
        pltpu.make_async_copy(sol_ref, sol_out, sems.at[0]),
        pltpu.make_async_copy(res_ref, res_out, sems.at[1]),
    ]
    for copy in copies:
        copy.start()
    for copy in copies:
        copy.wait()


def solution(mesh):
    n = mesh.shape["dom"]
    g1 = next(g for g in range(1, n + 1) if n % g == 0 and g * g >= n)
    g2 = n // g1

    def shards(rs, em, fm, si, sc, mass, absorb, imp):
        trace, own = rs.shape
        sides, elements = fm.shape
        blocks, width = si.shape[1:]
        pad = -(-trace // 8) * 8
        rows_own = own // WIDE * pad
        rows_ghost = blocks * width // WIDE * pad
        picks = sides * elements
        dofs = sides * trace
        cfg = (n, g1, g2, trace, sides, elements, own, blocks, width)
        dma = pltpu.SemaphoreType.DMA
        vmem = pl.BlockSpec(memory_space=pltpu.VMEM)
        sol, res = pl.pallas_call(
            functools.partial(kernel, cfg),
            out_shape=[pltpu.VMEM(rs.shape, F32)] * 2,
            in_specs=[pl.BlockSpec(memory_space=pltpu.HBM)] * 8,
            out_specs=[vmem] * 2,
            scratch_shapes=[
                pltpu.VMEM(rs.shape, F32),
                pltpu.VMEM(fm.shape, jnp.int32),
                pltpu.VMEM(si.shape, jnp.int32),
                pltpu.VMEM(sc.shape, jnp.int32),
                pltpu.VMEM((1, own), F32),
                pltpu.VMEM((1, own), jnp.int32),
                pltpu.VMEM((1, own), F32),
                pltpu.VMEM((dofs, dofs, elements), BF16),
                pltpu.VMEM((WIDE, picks), BF16),
                pltpu.VMEM((WIDE, blocks * width), BF16),
                pltpu.VMEM((2, rows_ghost, WIDE), F32),
                pltpu.VMEM((2, rows_ghost, WIDE), F32),
                pltpu.VMEM((2, rows_ghost, WIDE), F32),
                pltpu.VMEM((2, rows_ghost, WIDE), F32),
                pltpu.VMEM((sides, pad, elements), F32),
                pltpu.VMEM((dofs + 8, elements), F32),
                pltpu.VMEM((3 * rows_own, picks), BF16),
                pltpu.VMEM((3 * rows_ghost, picks), BF16),
                pltpu.VMEM((rows_own, WIDE), F32),
                pltpu.VMEM((rows_own, WIDE), F32),
                pltpu.VMEM((g1, 2, LANES), F32),
                pltpu.VMEM((g2, 2, LANES), F32),
                pltpu.VMEM((n, 2, LANES), F32),
                dma((7,)), dma((sides,)),
                dma((2, blocks)), dma((2, blocks)), dma((2, blocks)), dma((2, blocks)),
                dma((g1,)), dma((g1,)), dma((g2,)), dma((g2,)), dma((n,)), dma((n,)),
            ],
            compiler_params=pltpu.CompilerParams(
                collective_id=0, has_side_effects=True, vmem_limit_bytes=62 * 1024 * 1024
            ),
        )(rs, em, fm, si, sc, mass.reshape(1, own), absorb.reshape(1, own), imp.reshape(1, own))
        return pl.pallas_call(
            put_out,
            out_shape=[jax.ShapeDtypeStruct(rs.shape, F32)] * 2,
            in_specs=[vmem] * 2,
            out_specs=[pl.BlockSpec(memory_space=pltpu.HBM)] * 2,
            scratch_shapes=[dma((2,))],
            compiler_params=pltpu.CompilerParams(vmem_limit_bytes=8 * 1024 * 1024),
        )(sol, res)

    placed = (
        P(None, "dom"),
        P(None, None, "dom"),
        P(None, "dom"),
        P("dom", None, None),
        P("dom", None),
        P("dom"),
        P("dom"),
        P("dom"),
    )
    return jax.shard_map(
        shards,
        mesh=mesh,
        in_specs=placed,
        out_specs=(P(None, "dom"), P(None, "dom")),
        check_vma=False,
    )
```

profile of v0, /device:TPU:0, one launch (start us, length us, event | category | flops | bytes accessed | tf_op | source)
XLA Modules:
  0.0 32.1 jit_solution(11661342434152883665)
XLA Ops:
  0.6 30.8 %shard_map.95 = (f32[18,1024]{1,0:T(8,128)S(1)}, f32[18,1024]{1,0:T(8,128)S(1)}) custom-call(f32[18,1024]{1,0:T(8,128)} %rs_in.1, bf16[72,72,512]{2,1,0:T(8,128)(2,1)} %em_ref.1, s32[4,512]{1,0:T(4,128)} %fm_in.1, s32[1,4,128]{2,1,0:T(4,128)} %si_in.1, s32[1,4]{1,0:T(1,128)} %sc_in.1, f32[1,1024]{1,0:T(1,128)} %bitcast.3, s32[1,1024]{1,0:T(1,128)} %bitcast.4, ...), custom_call_target="tpu_custom_call" | custom-call | tf_op jit(solution)/shard_map/pallas_call | solution.py:390
  31.4 0.7 %shard_map.96 = (f32[18,1024]{1,0:T(8,128)}, f32[18,1024]{1,0:T(8,128)}) custom-call(f32[18,1024]{1,0:T(8,128)S(1)} %get-tuple-element.4.sol_ref, f32[18,1024]{1,0:T(8,128)S(1)} %get-tuple-element.5.res_ref), custom_call_target="tpu_custom_call" | custom-call | tf_op jit(solution)/shard_map/pallas_call | solution.py:427
where the time goes:
time: 32.2 us; the launch traced here: 32.1 us
  Pallas kernels  31.4 us (98%)
  between operations  0.64 us (2%)
    pallas_call x1, Pallas kernels, shards(): pl.pallas_call(functools.partial(kernel, cfg), out_shape=[pltpu.VMEM(rs.s...  30.8 us
    pallas_call x1, Pallas kernels, shards(): pl.pallas_call(put_out, out_shape=[jax.ShapeDtypeStruct(rs.shape, F32)] *...  0.69 us

commit v1 on v0

v1 whole, which is shorter than its diff:
```python
import functools
import jax
import jax.numpy as jnp
from jax import lax
from jax.experimental import pallas as pl
from jax.experimental.pallas import tpu as pltpu
from jax.sharding import PartitionSpec as P

LANES = 128
WIDE = 256
MESH = pl.DeviceIdType.MESH
F32 = jnp.float32
BF16 = jnp.bfloat16


def offset_list(block_count):
    half_count = block_count // 2
    return [
        block_index - half_count if block_index < half_count else block_index - half_count + 1
        for block_index in range(block_count)
    ]


def split2(x):
    high = x.astype(BF16)
    low = (x - high.astype(F32)).astype(BF16)
    return jnp.concatenate([high, low], axis=0)


def sum2(x):
    rows = x.shape[0] // 2
    return x[:rows] + x[rows:]


def dot(a, b):
    return lax.dot_general(a, b, (((1,), (0,)), ((), ())), preferred_element_type=F32)


def dot_nt(a, b):
    return lax.dot_general(a, b, (((1,), (1,)), ((), ())), preferred_element_type=F32)


def lane_pick(x, index):
    return jnp.take_along_axis(x, index, axis=1, mode="promise_in_bounds")


def kernel(
    cfg,
    rs_in, em_ref, fm_in, si_in, sc_in, mass_in, absorb_in, imp_in,
    sol_ref, res_ref,
    rs_ref, fm_ref, si_ref, sc_ref, mass_ref, absorb_ref, imp_ref,
    em_buf, pick_map, send_map, same_map, h_send, h_recv,
    own_buf, picked, x_high, x_low, prod, sums,
    in_sem, em_sem, h_send_sem, h_recv_sem, s_send_sem, s_recv_sem,
):
    n, g1, g2, trace, sides, elements, own, blocks, width = cfg
    offsets = offset_list(blocks)
    pad = -(-trace // 8) * 8
    dofs = sides * trace
    own_hi = own // WIDE
    ghost = blocks * width
    ghost_hi = ghost // WIDE
    own_tiles, ghost_tiles = own // LANES, ghost // LANES
    tiles = elements // LANES
    me = lax.axis_index("dom")
    block_of, in_block = me // g1, lax.rem(me, g1)

    barrier = pltpu.get_barrier_semaphore()
    waits = jnp.int32((g1 - 1) + (g2 - 1))
    near = jnp.int32(0)
    for o in offsets:
        there = me + o
        inside = (there >= 0) & (there < n)
        near = near + inside.astype(jnp.int32)

        @pl.when(inside)
        def _():
            pl.semaphore_signal(barrier, inc=1, device_id=(there,), device_id_type=MESH)

    waits = waits + near

    def peer1(d):
        return block_of * g1 + lax.rem(in_block + d, g1)

    def peer2(d):
        return lax.rem(block_of + d, g2) * g1 + in_block

    for d in range(1, g1):
        pl.semaphore_signal(barrier, inc=1, device_id=(peer1(d),), device_id_type=MESH)
    for d in range(1, g2):
        pl.semaphore_signal(barrier, inc=1, device_id=(peer2(d),), device_id_type=MESH)

    in_copies = [
        pltpu.make_async_copy(source, target, in_sem.at[i])
        for i, (source, target) in enumerate(
            (
                (rs_in, rs_ref), (si_in, si_ref), (sc_in, sc_ref), (fm_in, fm_ref),
                (mass_in, mass_ref), (absorb_in, absorb_ref), (imp_in, imp_ref),
            )
        )
    ]
    for copy in in_copies:
        copy.start()
    for t in range(tiles):
        pltpu.make_async_copy(
            em_ref.at[:, pl.ds(t * LANES, LANES)], em_buf.at[t], em_sem
        ).start()

    def piece(ref, i, k):
        return ref.at[i, :, pl.ds(k * width, width)]

    def halo(i, k, step):
        there = me + step
        copy = pltpu.make_async_remote_copy(
            src_ref=piece(h_send, i, k), dst_ref=piece(h_recv, i, k),
            send_sem=h_send_sem, recv_sem=h_recv_sem.at[i],
            device_id=(there,), device_id_type=MESH,
        )
        return copy, (there >= 0) & (there < n)

    far_first = sorted(range(blocks), key=lambda k: -abs(offsets[k]))

    def step_of(i, k):
        return offsets[k] if i % 2 == 0 else -offsets[k]

    def start_all(i):
        for k in far_first:
            copy, to = halo(i, k, step_of(i, k))
            pl.when(to)(copy.start)

    def wait_near(view, sem):
        for count in range(1, blocks + 1):

            @pl.when(near == count)
            def _():
                ref = view(count)
                pltpu.make_async_copy(ref, ref, sem).wait()

    def wait_recv(i):
        wait_near(lambda count: h_recv.at[i, :, pl.ds(0, count * width)], h_recv_sem.at[i])

    for copy in in_copies[:3]:
        copy.wait()

    row_live = lax.broadcasted_iota(jnp.int32, (8, LANES), 0) < trace - (pad - 8)
    own_buf[...] = jnp.zeros_like(own_buf)
    own_buf[0, 0:trace, :] = rs_ref[...]
    slot_iota = lax.broadcasted_iota(jnp.int32, (1, width), 1)
    alive = [slot_iota < sc_ref[0:1, k : k + 1] for k in range(blocks)]
    send_index = [si_ref[0, k : k + 1, :] for k in range(blocks)]

    def pick_tile(source, first_tile, count, index, value):
        low = jnp.broadcast_to(index & (LANES - 1), (pad, LANES))
        high = jnp.broadcast_to(index >> 7, (pad, LANES))
        for h in range(count):
            got = lane_pick(source(h), low)
            value = jnp.where(high == first_tile + h, got, value)
        return value

    def own_tile(rnd):
        return lambda h: own_buf[rnd, :, h * LANES : (h + 1) * LANES]

    def send_values(rnd, k):
        value = pick_tile(
            own_tile(rnd), 0, own_tiles, send_index[k], jnp.zeros((pad, LANES), F32)
        )
        return jnp.where(alive[k], value, 0.0)

    for k in range(blocks):
        h_send[0, :, k * width : (k + 1) * width] = send_values(0, k)
    for k in range(blocks):
        for i in range(4):
            came = me - step_of(i, k)

            @pl.when((came < 0) | (came >= n))
            def _():
                h_recv[i, :, k * width : (k + 1) * width] = jnp.zeros((pad, width), F32)

    pl.semaphore_wait(barrier, waits)
    start_all(0)

    for copy in in_copies[3:]:
        copy.wait()

    def face_index(t, s):
        return fm_ref[s : s + 1, t * LANES : (t + 1) * LANES]

    def pick_own(rnd):
        for t in range(tiles):
            for s in range(sides):
                picked[rnd, t, s] = pick_tile(
                    own_tile(rnd), 0, own_tiles, face_index(t, s), jnp.zeros((pad, LANES), F32)
                )

    pick_own(0)

    lo_iota = lax.broadcasted_iota(jnp.int32, (WIDE, LANES), 0)

    def one_hot(test):
        return jnp.where(test, 1.0, 0.0).astype(BF16)

    for t in range(tiles):
        for s in range(sides):
            lane = (t * sides + s) * LANES
            low = face_index(t, s) & (WIDE - 1)
            pick_map[:, lane : lane + LANES] = one_hot(lo_iota == low)
    for k in range(blocks):
        low = jnp.where(alive[k], send_index[k] & (WIDE - 1), -1)
        send_map[:, k * width : (k + 1) * width] = one_hot(lo_iota == low)
    for a in range(blocks):
        index = jnp.where(alive[a], send_index[a], -2).astype(F32)
        column = jnp.transpose(jnp.broadcast_to(index, (width, width)))
        for k in range(blocks):
            row = jnp.where(alive[k], send_index[k], -1).astype(F32)
            same_map[a * width : (a + 1) * width, k * width : (k + 1) * width] = one_hot(
                column == row
            )
    prod[...] = jnp.zeros_like(prod)
    diag_row = mass_ref[...] + absorb_ref[...].astype(F32) * imp_ref[...]

    pairs = dofs // 2
    body = dofs - 8

    def product(t):
        def row_at(ref, j):
            at = j // trace * pad + j % trace
            return jnp.broadcast_to(ref[t, at : at + 1, :], (8, LANES))

        def run(first, blocks, inputs):
            total = [None] * blocks
            for jj in range(pairs):
                at = jj * 2 * dofs + first
                high, low = (inputs(ref, jj).astype(BF16) for ref in (x_high, x_low))
                for i in range(blocks):
                    matrix = em_buf[t, at + i * 16 : at + i * 16 + 16, :]
                    for x in (high, low):
                        term = matrix.astype(F32) * x.astype(F32)
                        total[i] = term if jj == 0 and x is high else total[i] + term
            return total

        def rows(first, second):
            return lambda ref, jj: jnp.concatenate(
                [row_at(ref, 2 * jj + first), row_at(ref, 2 * jj + second)], axis=0
            )

        even = run(0, body // 16, rows(0, 0))
        odd = run(dofs + 8, body // 16, rows(1, 1))
        mixed = run(body, 1, rows(0, 1))[0]
        return jnp.concatenate(even + [mixed[:8]], axis=0) + jnp.concatenate(
            [mixed[8:]] + odd, axis=0
        )

    def side_values(rnd, t, s):
        value = prod[rnd, t, s * trace : s * trace + pad, :]
        return jnp.concatenate(
            [value[: pad - 8], jnp.where(row_live, value[pad - 8 :], 0.0)], axis=0
        )

    def spread(rnd, t, first_hi, count):
        parts = []
        for s in range(sides):
            value = side_values(rnd, t, s)
            high = jnp.broadcast_to(face_index(t, s) >> 8, (pad, LANES))
            parts.append(
                split2(
                    jnp.concatenate(
                        [jnp.where(high == first_hi + h, value, 0.0) for h in range(count)], axis=0
                    )
                )
            )
        lane = t * sides * LANES
        return dot_nt(
            jnp.concatenate(parts, axis=1), pick_map[:, lane : lane + sides * LANES]
        )

    def elements_of(rnd):
        source = 2 * rnd
        ghost_total = None
        for t in range(tiles):
            for s in range(sides):
                value = pick_tile(
                    lambda h: h_recv[source, :, h * LANES : (h + 1) * LANES],
                    own_tiles, ghost_tiles, face_index(t, s), picked[rnd, t, s],
                )
                picked[rnd, t, s] = value
                high = value.astype(BF16).astype(F32)
                x_high[t, s * pad : (s + 1) * pad, :] = high
                x_low[t, s * pad : (s + 1) * pad, :] = value - high
            prod[rnd, t, 0:dofs, :] = product(t)
        for t in range(tiles):
            part = spread(rnd, t, own_hi, ghost_hi)
            ghost_total = part if ghost_total is None else ghost_total + part
        ghost_total = sum2(ghost_total)
        for h in range(ghost_hi):
            h_send[source + 1, :, h * WIDE : (h + 1) * WIDE] = ghost_total[h * pad : (h + 1) * pad]

    def own_sums(rnd):
        total = None
        for t in range(tiles):
            part = spread(rnd, t, 0, own_hi)
            total = part if total is None else total + part
        total = sum2(total)
        for h in range(own_hi):
            lanes = slice(h * WIDE, (h + 1) * WIDE)
            own_buf[rnd + 1, :, lanes] = (
                total[h * pad : (h + 1) * pad] + own_buf[rnd, :, lanes] * diag_row[:, lanes]
            )

    def add_returned(rnd):
        parts = []
        for k in range(blocks):
            value = h_recv[2 * rnd + 1, :, k * width : (k + 1) * width]
            high = jnp.broadcast_to(send_index[k] >> 8, (pad, LANES))
            parts.append(
                split2(
                    jnp.concatenate(
                        [jnp.where(high == i, value, 0.0) for i in range(own_hi)], axis=0
                    )
                )
            )
        total = sum2(dot_nt(jnp.concatenate(parts, axis=1), send_map[...]))
        for h in range(own_hi):
            lanes = slice(h * WIDE, (h + 1) * WIDE)
            own_buf[rnd + 1, :, lanes] += total[h * pad : (h + 1) * pad]

    def sum_copy(target, slot_here, slot_there, sem):
        return pltpu.make_async_remote_copy(
            src_ref=sums.at[slot_here], dst_ref=sums.at[slot_there],
            send_sem=s_send_sem, recv_sem=s_recv_sem.at[sem],
            device_id=(target,), device_id_type=MESH,
        )

    def sum_wait(first, count, sem):
        ref = sums.at[pl.ds(first, count)]
        pltpu.make_async_copy(ref, ref, sem).wait()

    def lane_sums(x):
        total = jnp.sum(x, axis=0, keepdims=True)
        while total.shape[1] > LANES:
            half = total.shape[1] // 2
            total = total[:, :half] + total[:, half:]
        return total

    def totals(parts):
        total = jnp.sum(jnp.sum(parts, axis=0), axis=1, keepdims=True)
        return total[0:1], total[1:2]

    def begin_sum(x, y):
        sums[in_block] = jnp.concatenate([x, y], axis=0)
        for d in range(1, g1):
            sum_copy(peer1(d), in_block, in_block, 0).start()

    def middle_sum():
        sum_wait(0, g1 - 1, s_recv_sem.at[0])
        sums[g1 + block_of] = jnp.sum(sums[0:g1], axis=0)
        for d in range(1, g2):
            sum_copy(peer2(d), g1 + block_of, g1 + block_of, 1).start()

    def end_sum():
        sum_wait(0, g2 - 1, s_recv_sem.at[1])
        return totals(sums[g1 : g1 + g2])

    def begin_straight(x, y):
        base = g1 + g2
        sums[base] = jnp.concatenate([x, y], axis=0)
        for d in sorted(range(1, n), key=lambda d: abs(2 * d - n)):
            sum_copy(lax.rem(me + d, n), base, base + d, 2).start()

    def end_straight():
        sum_wait(0, n - 1, s_recv_sem.at[2])
        return totals(sums[g1 + g2 : g1 + g2 + n])

    pltpu.make_async_copy(em_buf, em_buf, em_sem).wait()
    wait_recv(0)
    elements_of(0)
    start_all(1)
    b = own_buf[0]
    energy = None
    for t in range(tiles):
        for s in range(sides):
            term = picked[0, t, s] * side_values(0, t, s)
            energy = term if energy is None else energy + term
    begin_sum(lane_sums(b * b), lane_sums(energy) + lane_sums(b * b * diag_row))
    own_sums(0)
    partial_send = [send_values(1, k) for k in range(blocks)]
    for k in range(blocks):
        h_send[2, :, k * width : (k + 1) * width] = partial_send[k]
    wait_recv(1)
    shared = sum2(dot(split2(h_recv[1]), same_map[...]))
    h_send[2] = h_send[2] + shared
    start_all(2)
    middle_sum()
    add_returned(0)
    pick_own(1)

    wait_recv(2)
    elements_of(1)
    start_all(3)
    rr, curve = end_sum()
    step0 = rr / curve
    energy = None
    for t in range(tiles):
        for s in range(sides):
            left = picked[0, t, s] - step0 * picked[1, t, s]
            right = side_values(0, t, s) - step0 * side_values(1, t, s)
            term = left * right
            energy = term if energy is None else energy + term
    r1 = own_buf[0] - step0 * own_buf[1]
    r1_square = r1 * r1
    begin_straight(lane_sums(r1_square), lane_sums(energy) + lane_sums(r1_square * diag_row))
    own_sums(1)
    wait_recv(3)
    add_returned(1)
    new, curve = end_straight()
    beta = new / rr
    step1 = new / (curve - beta * new / step0)
    b, q, w = own_buf[0, 0:trace], own_buf[1, 0:trace], own_buf[2, 0:trace]
    r1 = b - step0 * q
    sol_ref[...] = step0 * b + step1 * (r1 + beta * b)
    res_ref[...] = r1 - step1 * (q - step0 * w + beta * q)
    wait_near(lambda count: h_send.at[:, :, pl.ds(0, count * width)], h_send_sem)
    sum_wait(0, (g1 - 1) + (g2 - 1) + (n - 1), s_send_sem)


def put_out(sol_ref, res_ref, sol_out, res_out, sems):
    copies = [
        pltpu.make_async_copy(sol_ref, sol_out, sems.at[0]),
        pltpu.make_async_copy(res_ref, res_out, sems.at[1]),
    ]
    for copy in copies:
        copy.start()
    for copy in copies:
        copy.wait()


def solution(mesh):
    n = mesh.shape["dom"]
    g1 = next(g for g in range(1, n + 1) if n % g == 0 and g * g >= n)
    g2 = n // g1

    def shards(rs, em, fm, si, sc, mass, absorb, imp):
        trace, own = rs.shape
        sides, elements = fm.shape
        blocks, width = si.shape[1:]
        pad = -(-trace // 8) * 8
        dofs = sides * trace
        tiles = elements // LANES
        ghost = blocks * width
        assert width == LANES and dofs % 16 == 8
        cfg = (n, g1, g2, trace, sides, elements, own, blocks, width)
        dma = pltpu.SemaphoreType.DMA
        vmem = pl.BlockSpec(memory_space=pltpu.VMEM)
        sol, res = pl.pallas_call(
            functools.partial(kernel, cfg),
            out_shape=[pltpu.VMEM(rs.shape, F32)] * 2,
            in_specs=[pl.BlockSpec(memory_space=pltpu.HBM)] * 8,
            out_specs=[vmem] * 2,
            scratch_shapes=[
                pltpu.VMEM(rs.shape, F32),
                pltpu.VMEM(fm.shape, jnp.int32),
                pltpu.VMEM(si.shape, jnp.int32),
                pltpu.VMEM(sc.shape, jnp.int32),
                pltpu.VMEM((1, own), F32),
                pltpu.VMEM((1, own), jnp.int32),
                pltpu.VMEM((1, own), F32),
                pltpu.VMEM((tiles, dofs * dofs, LANES), BF16),
                pltpu.VMEM((WIDE, sides * elements), BF16),
                pltpu.VMEM((WIDE, ghost), BF16),
                pltpu.VMEM((ghost, ghost), BF16),
                pltpu.VMEM((4, pad, ghost), F32),
                pltpu.VMEM((4, pad, ghost), F32),
                pltpu.VMEM((3, pad, own), F32),
                pltpu.VMEM((2, tiles, sides, pad, LANES), F32),
                pltpu.VMEM((tiles, sides * pad, LANES), F32),
                pltpu.VMEM((tiles, sides * pad, LANES), F32),
                pltpu.VMEM((2, tiles, dofs + 8, LANES), F32),
                pltpu.VMEM((g1 + g2 + n, 2, LANES), F32),
                dma((7,)), dma(()), dma(()), dma((4,)), dma(()), dma((3,)),
            ],
            compiler_params=pltpu.CompilerParams(
                collective_id=0, has_side_effects=True, vmem_limit_bytes=62 * 1024 * 1024
            ),
        )(
            rs, em.reshape(dofs * dofs, elements), fm, si, sc,
            mass.reshape(1, own), absorb.reshape(1, own), imp.reshape(1, own),
        )
        return pl.pallas_call(
            put_out,
            out_shape=[jax.ShapeDtypeStruct(rs.shape, F32)] * 2,
            in_specs=[vmem] * 2,
            out_specs=[pl.BlockSpec(memory_space=pltpu.HBM)] * 2,
            scratch_shapes=[dma((2,))],
            compiler_params=pltpu.CompilerParams(vmem_limit_bytes=8 * 1024 * 1024),
        )(sol, res)

    placed = (
        P(None, "dom"),
        P(None, None, "dom"),
        P(None, "dom"),
        P("dom", None, None),
        P("dom", None),
        P("dom"),
        P("dom"),
        P("dom"),
    )
    return jax.shard_map(
        shards,
        mesh=mesh,
        in_specs=placed,
        out_specs=(P(None, "dom"), P(None, "dom")),
        check_vma=False,
    )
```

time: 32.2 us -> 24.9 us (0.77)
  Pallas kernels: 31.4 us -> 24.2 us
    pallas_call x1, Pallas kernels: 30.8 us -> 23.5 us  [shards(): pl.pallas_call(functools.partial(kernel, cfg), out_shape=[pltpu.VMEM(rs.s...]
where the time goes in v1:
time: 24.9 us; the launch traced here: 24.8 us
  Pallas kernels  24.2 us (97%)
  between operations  0.64 us (3%)
    pallas_call x1, Pallas kernels, shards(): pl.pallas_call(functools.partial(kernel, cfg), out_shape=[pltpu.VMEM(rs.s...  23.5 us
    pallas_call x1, Pallas kernels, shards(): pl.pallas_call(put_out, out_shape=[jax.ShapeDtypeStruct(rs.shape, F32)] *...  0.69 us

profile of v1, /device:TPU:0, one launch (start us, length us, event | category | flops | bytes accessed | tf_op | source)
XLA Modules:
  0.0 24.8 jit_solution(3114115078676137229)
XLA Ops:
  0.6 23.5 %shard_map.95 = (f32[18,1024]{1,0:T(8,128)S(1)}, f32[18,1024]{1,0:T(8,128)S(1)}) custom-call(f32[18,1024]{1,0:T(8,128)} %rs_in.1, bf16[5184,512]{1,0:T(8,128)(2,1)} %bitcast.4, s32[4,512]{1,0:T(4,128)} %fm_in.1, s32[1,4,128]{2,1,0:T(4,128)} %si_in.1, s32[1,4]{1,0:T(1,128)} %sc_in.1, f32[1,1024]{1,0:T(1,128)} %bitcast.5, s32[1,1024]{1,0:T(1,128)} %bitcast.6, ...), custom_call_target="tpu_custom_call" | custom-call | tf_op jit(solution)/shard_map/pallas_call | solution.py:453
  24.1 0.7 %shard_map.96 = (f32[18,1024]{1,0:T(8,128)}, f32[18,1024]{1,0:T(8,128)}) custom-call(f32[18,1024]{1,0:T(8,128)S(1)} %get-tuple-element.4.sol_ref, f32[18,1024]{1,0:T(8,128)S(1)} %get-tuple-element.5.res_ref), custom_call_target="tpu_custom_call" | custom-call | tf_op jit(solution)/shard_map/pallas_call | solution.py:487

commit v2 on v1

--- a/solution.py
+++ b/solution.py
@@ -49,9 +49,9 @@
     rs_in, em_ref, fm_in, si_in, sc_in, mass_in, absorb_in, imp_in,
     sol_ref, res_ref,
     rs_ref, fm_ref, si_ref, sc_ref, mass_ref, absorb_ref, imp_ref,
-    em_buf, pick_map, send_map, same_map, h_send, h_recv,
+    em_buf, pick_map, send_map, same_map, pick_same, h_send, h_recv, x_recv,
     own_buf, picked, x_high, x_low, prod, sums,
-    in_sem, em_sem, h_send_sem, h_recv_sem, s_send_sem, s_recv_sem,
+    in_sem, em_sem, h_send_sem, h_recv_sem, s_send_sem, s_recv_sem, ready,
 ):
     n, g1, g2, trace, sides, elements, own, blocks, width = cfg
     offsets = offset_list(blocks)
@@ -67,17 +67,14 @@
 
     barrier = pltpu.get_barrier_semaphore()
     waits = jnp.int32((g1 - 1) + (g2 - 1))
-    near = jnp.int32(0)
     for o in offsets:
         there = me + o
         inside = (there >= 0) & (there < n)
-        near = near + inside.astype(jnp.int32)
+        waits = waits + inside.astype(jnp.int32)
 
         @pl.when(inside)
         def _():
             pl.semaphore_signal(barrier, inc=1, device_id=(there,), device_id_type=MESH)
-
-    waits = waits + near
 
     def peer1(d):
         return block_of * g1 + lax.rem(in_block + d, g1)
@@ -106,38 +103,70 @@
             em_ref.at[:, pl.ds(t * LANES, LANES)], em_buf.at[t], em_sem
         ).start()
 
-    def piece(ref, i, k):
-        return ref.at[i, :, pl.ds(k * width, width)]
-
-    def halo(i, k, step):
-        there = me + step
-        copy = pltpu.make_async_remote_copy(
-            src_ref=piece(h_send, i, k), dst_ref=piece(h_recv, i, k),
-            send_sem=h_send_sem, recv_sem=h_recv_sem.at[i],
-            device_id=(there,), device_id_type=MESH,
-        )
-        return copy, (there >= 0) & (there < n)
+    def valid(device):
+        return (device >= 0) & (device < n)
+
+    def send_piece(source, target, device, i):
+        return pltpu.make_async_remote_copy(
+            src_ref=source, dst_ref=target,
+            send_sem=h_send_sem.at[int(i == 2)], recv_sem=h_recv_sem.at[i],
+            device_id=(device,), device_id_type=MESH,
+        )
 
     far_first = sorted(range(blocks), key=lambda k: -abs(offsets[k]))
 
     def step_of(i, k):
-        return offsets[k] if i % 2 == 0 else -offsets[k]
+        return offsets[k] if i == 0 else -offsets[k]
 
     def start_all(i):
         for k in far_first:
-            copy, to = halo(i, k, step_of(i, k))
-            pl.when(to)(copy.start)
-
-    def wait_near(view, sem):
-        for count in range(1, blocks + 1):
-
-            @pl.when(near == count)
+            there = me + step_of(i, k)
+            copy = send_piece(h_send.at[i, k], h_recv.at[i, k], there, i)
+            pl.when(valid(there))(copy.start)
+
+    def relays():
+        pairs = [(k, c) for k in range(blocks) for c in range(blocks) if c != k]
+        pairs.sort(key=lambda kc: -abs(offsets[kc[1]] - offsets[kc[0]]))
+        for k, c in pairs:
+            owner = me - offsets[k]
+            there = owner + offsets[c]
+            copy = send_piece(h_send.at[1, k], x_recv.at[c * blocks + k], there, 2)
+            yield copy, valid(owner) & valid(there)
+
+    def owners():
+        for k in far_first:
+            there = me + offsets[k]
+            copy = send_piece(h_send.at[2, k], x_recv.at[k * blocks + k], there, 2)
+            yield copy, valid(there)
+
+    def count_of(device, as_count):
+        near_count, cross_count = 0, 0
+        for k in range(blocks):
+            owner = device - offsets[k]
+            near_count += as_count(valid(owner))
+            for c in range(blocks):
+                other = owner + offsets[c]
+                cross_count += as_count(valid(owner) & valid(other))
+        return near_count, cross_count
+
+    near, cross = count_of(me, lambda test: test.astype(jnp.int32))
+    counts = [count_of(device, int) for device in range(n)]
+
+    def wait_count(number, choices, view, sem):
+        for count in sorted(set(choices)):
+
+            @pl.when(number == count)
             def _():
                 ref = view(count)
                 pltpu.make_async_copy(ref, ref, sem).wait()
 
+    near_choices = [pair[0] for pair in counts]
+    cross_choices = [pair[1] for pair in counts]
+
     def wait_recv(i):
-        wait_near(lambda count: h_recv.at[i, :, pl.ds(0, count * width)], h_recv_sem.at[i])
+        wait_count(
+            near, near_choices, lambda count: h_recv.at[i, pl.ds(0, count)], h_recv_sem.at[i]
+        )
 
     for copy in in_copies[:3]:
         copy.wait()
@@ -166,18 +195,41 @@
         )
         return jnp.where(alive[k], value, 0.0)
 
+    shared_index = [jnp.where(alive[k], send_index[k], -1).astype(F32) for k in range(blocks)]
     for k in range(blocks):
-        h_send[0, :, k * width : (k + 1) * width] = send_values(0, k)
-    for k in range(blocks):
-        for i in range(4):
-            came = me - step_of(i, k)
-
-            @pl.when((came < 0) | (came >= n))
+        h_send[0, k] = send_values(0, k)
+        for c in range(blocks):
+            h_send[0, k, trace + c : trace + c + 1, :] = shared_index[c]
+
+    @pl.when(cross < blocks * blocks)
+    def _():
+        empty = jnp.zeros((pad, width), F32)
+        no_index = jnp.where(
+            lax.broadcasted_iota(jnp.int32, (pad, width), 0) < trace, 0.0, -1.0
+        )
+        for k in range(blocks):
+            owner = me - offsets[k]
+
+            @pl.when(~valid(owner))
             def _():
-                h_recv[i, :, k * width : (k + 1) * width] = jnp.zeros((pad, width), F32)
+                h_recv[0, k] = no_index
+
+            for i in (1, 3):
+
+                @pl.when(~valid(me - step_of(i, k)))
+                def _():
+                    h_recv[i, k] = empty
+
+            for c in range(blocks):
+
+                @pl.when(~(valid(owner) & valid(owner + offsets[c])))
+                def _():
+                    x_recv[k * blocks + c] = empty
 
     pl.semaphore_wait(barrier, waits)
     start_all(0)
+    for d in range(1, g1):
+        pl.semaphore_signal(ready, inc=1, device_id=(peer1(d),), device_id_type=MESH)
 
     for copy in in_copies[3:]:
         copy.wait()
@@ -188,7 +240,7 @@
     def pick_own(rnd):
         for t in range(tiles):
             for s in range(sides):
-                picked[rnd, t, s] = pick_tile(
+                picked[t, s] = pick_tile(
                     own_tile(rnd), 0, own_tiles, face_index(t, s), jnp.zeros((pad, LANES), F32)
                 )
 
@@ -207,16 +259,28 @@
     for k in range(blocks):
         low = jnp.where(alive[k], send_index[k] & (WIDE - 1), -1)
         send_map[:, k * width : (k + 1) * width] = one_hot(lo_iota == low)
-    for a in range(blocks):
-        index = jnp.where(alive[a], send_index[a], -2).astype(F32)
-        column = jnp.transpose(jnp.broadcast_to(index, (width, width)))
-        for k in range(blocks):
-            row = jnp.where(alive[k], send_index[k], -1).astype(F32)
-            same_map[a * width : (a + 1) * width, k * width : (k + 1) * width] = one_hot(
-                column == row
-            )
     prod[...] = jnp.zeros_like(prod)
     diag_row = mass_ref[...] + absorb_ref[...].astype(F32) * imp_ref[...]
+
+    def column_of(row):
+        dead_apart = jnp.where(row < 0.0, -2.0, row)
+        return jnp.transpose(jnp.broadcast_to(dead_apart, (width, width)))
+
+    def map_shared():
+        for k in range(blocks):
+            rows = [h_recv[0, k, trace + c : trace + c + 1, :] for c in range(blocks)]
+            for c in range(blocks):
+                same_map[k, c * width : (c + 1) * width, :] = one_hot(column_of(rows[c]) == rows[k])
+
+    def map_returned():
+        for k in range(blocks):
+            column = column_of(shared_index[k])
+            for t in range(tiles):
+                for s in range(sides):
+                    lane = (t * sides + s) * LANES
+                    pick_same[k * width : (k + 1) * width, lane : lane + LANES] = one_hot(
+                        column == face_index(t, s).astype(F32)
+                    )
 
     pairs = dofs // 2
     body = dofs - 8
@@ -250,16 +314,16 @@
             [mixed[8:]] + odd, axis=0
         )
 
-    def side_values(rnd, t, s):
-        value = prod[rnd, t, s * trace : s * trace + pad, :]
+    def side_values(t, s):
+        value = prod[t, s * trace : s * trace + pad, :]
         return jnp.concatenate(
             [value[: pad - 8], jnp.where(row_live, value[pad - 8 :], 0.0)], axis=0
         )
 
-    def spread(rnd, t, first_hi, count):
+    def spread(t, first_hi, count):
         parts = []
         for s in range(sides):
-            value = side_values(rnd, t, s)
+            value = side_values(t, s)
             high = jnp.broadcast_to(face_index(t, s) >> 8, (pad, LANES))
             parts.append(
                 split2(
@@ -274,30 +338,39 @@
         )
 
     def elements_of(rnd):
-        source = 2 * rnd
         ghost_total = None
         for t in range(tiles):
             for s in range(sides):
                 value = pick_tile(
-                    lambda h: h_recv[source, :, h * LANES : (h + 1) * LANES],
-                    own_tiles, ghost_tiles, face_index(t, s), picked[rnd, t, s],
+                    lambda h: h_recv[2 * rnd, h],
+                    own_tiles, ghost_tiles, face_index(t, s), picked[t, s],
                 )
-                picked[rnd, t, s] = value
+                picked[t, s] = value
                 high = value.astype(BF16).astype(F32)
                 x_high[t, s * pad : (s + 1) * pad, :] = high
                 x_low[t, s * pad : (s + 1) * pad, :] = value - high
-            prod[rnd, t, 0:dofs, :] = product(t)
+            prod[t, 0:dofs, :] = product(t)
         for t in range(tiles):
-            part = spread(rnd, t, own_hi, ghost_hi)
+            part = spread(t, own_hi, ghost_hi)
             ghost_total = part if ghost_total is None else ghost_total + part
         ghost_total = sum2(ghost_total)
-        for h in range(ghost_hi):
-            h_send[source + 1, :, h * WIDE : (h + 1) * WIDE] = ghost_total[h * pad : (h + 1) * pad]
+        per_wide = WIDE // width
+        for k in range(blocks):
+            h, lane = k // per_wide, k % per_wide * width
+            h_send[2 * rnd + 1, k] = ghost_total[h * pad : (h + 1) * pad, lane : lane + width]
+
+    def energy_of():
+        energy = None
+        for t in range(tiles):
+            for s in range(sides):
+                term = picked[t, s] * side_values(t, s)
+                energy = term if energy is None else energy + term
+        return lane_sums(energy)
 
     def own_sums(rnd):
         total = None
         for t in range(tiles):
-            part = spread(rnd, t, 0, own_hi)
+            part = spread(t, 0, own_hi)
             total = part if total is None else total + part
         total = sum2(total)
         for h in range(own_hi):
@@ -309,7 +382,7 @@
     def add_returned(rnd):
         parts = []
         for k in range(blocks):
-            value = h_recv[2 * rnd + 1, :, k * width : (k + 1) * width]
+            value = h_recv[2 * rnd + 1, k]
             high = jnp.broadcast_to(send_index[k] >> 8, (pad, LANES))
             parts.append(
                 split2(
@@ -323,17 +396,6 @@
             lanes = slice(h * WIDE, (h + 1) * WIDE)
             own_buf[rnd + 1, :, lanes] += total[h * pad : (h + 1) * pad]
 
-    def sum_copy(target, slot_here, slot_there, sem):
-        return pltpu.make_async_remote_copy(
-            src_ref=sums.at[slot_here], dst_ref=sums.at[slot_there],
-            send_sem=s_send_sem, recv_sem=s_recv_sem.at[sem],
-            device_id=(target,), device_id_type=MESH,
-        )
-
-    def sum_wait(first, count, sem):
-        ref = sums.at[pl.ds(first, count)]
-        pltpu.make_async_copy(ref, ref, sem).wait()
-
     def lane_sums(x):
         total = jnp.sum(x, axis=0, keepdims=True)
         while total.shape[1] > LANES:
@@ -341,85 +403,82 @@
             total = total[:, :half] + total[:, half:]
         return total
 
-    def totals(parts):
-        total = jnp.sum(jnp.sum(parts, axis=0), axis=1, keepdims=True)
-        return total[0:1], total[1:2]
-
-    def begin_sum(x, y):
-        sums[in_block] = jnp.concatenate([x, y], axis=0)
-        for d in range(1, g1):
-            sum_copy(peer1(d), in_block, in_block, 0).start()
-
-    def middle_sum():
-        sum_wait(0, g1 - 1, s_recv_sem.at[0])
-        sums[g1 + block_of] = jnp.sum(sums[0:g1], axis=0)
-        for d in range(1, g2):
-            sum_copy(peer2(d), g1 + block_of, g1 + block_of, 1).start()
+    def begin_sum(rows):
+        sums[me] = jnp.concatenate(rows, axis=0)
+        pl.semaphore_wait(ready, g1 - 1)
+        for d in range(n - 1):
+            pltpu.make_async_remote_copy(
+                src_ref=sums.at[me], dst_ref=sums.at[me],
+                send_sem=s_send_sem, recv_sem=s_recv_sem,
+                device_id=(d + (d >= me).astype(jnp.int32),), device_id_type=MESH,
+            ).start()
+
+    def sum_wait(sem):
+        ref = sums.at[pl.ds(0, n - 1)]
+        pltpu.make_async_copy(ref, ref, sem).wait()
 
     def end_sum():
-        sum_wait(0, g2 - 1, s_recv_sem.at[1])
-        return totals(sums[g1 : g1 + g2])
-
-    def begin_straight(x, y):
-        base = g1 + g2
-        sums[base] = jnp.concatenate([x, y], axis=0)
-        for d in sorted(range(1, n), key=lambda d: abs(2 * d - n)):
-            sum_copy(lax.rem(me + d, n), base, base + d, 2).start()
-
-    def end_straight():
-        sum_wait(0, n - 1, s_recv_sem.at[2])
-        return totals(sums[g1 + g2 : g1 + g2 + n])
+        sum_wait(s_recv_sem)
+        total = jnp.sum(jnp.sum(sums[...], axis=0), axis=1, keepdims=True)
+        return [total[i : i + 1] for i in range(4)]
 
     pltpu.make_async_copy(em_buf, em_buf, em_sem).wait()
     wait_recv(0)
     elements_of(0)
+    for copy, to in relays():
+        pl.when(to)(copy.start)
     start_all(1)
+    own_sums(0)
+    for k in range(blocks):
+        h_send[2, k] = send_values(1, k)
+    for copy, to in owners():
+        pl.when(to)(copy.start)
     b = own_buf[0]
-    energy = None
+    b_square = lane_sums(b * b)
+    b_energy = energy_of() + lane_sums(b * b * diag_row)
+    map_shared()
+    map_returned()
+    pick_own(1)
+
+    wait_recv(1)
+    wait_count(cross, cross_choices, lambda count: x_recv.at[pl.ds(0, count)], h_recv_sem.at[2])
+    for k in range(blocks):
+        parts = jnp.concatenate(
+            [h_send[1, k] if c == k else x_recv[k * blocks + c] for c in range(blocks)], axis=1
+        )
+        h_recv[2, k] = x_recv[k * blocks + k] + sum2(dot(split2(parts), same_map[k]))
+    returned = split2(jnp.concatenate([h_recv[1, k] for k in range(blocks)], axis=1))
     for t in range(tiles):
+        lane = t * sides * LANES
+        extra = sum2(dot(returned, pick_same[:, lane : lane + sides * LANES]))
         for s in range(sides):
-            term = picked[0, t, s] * side_values(0, t, s)
-            energy = term if energy is None else energy + term
-    begin_sum(lane_sums(b * b), lane_sums(energy) + lane_sums(b * b * diag_row))
-    own_sums(0)
-    partial_send = [send_values(1, k) for k in range(blocks)]
-    for k in range(blocks):
-        h_send[2, :, k * width : (k + 1) * width] = partial_send[k]
-    wait_recv(1)
-    shared = sum2(dot(split2(h_recv[1]), same_map[...]))
-    h_send[2] = h_send[2] + shared
-    start_all(2)
-    middle_sum()
+            picked[t, s] += extra[:, s * LANES : (s + 1) * LANES]
     add_returned(0)
-    pick_own(1)
-
-    wait_recv(2)
+    q = own_buf[1]
+    q_square = lane_sums(q * q)
+    q_diagonal = lane_sums(q * q * diag_row)
+
     elements_of(1)
+    begin_sum([b_square, b_energy, q_square, energy_of() + q_diagonal])
     start_all(3)
-    rr, curve = end_sum()
-    step0 = rr / curve
-    energy = None
-    for t in range(tiles):
-        for s in range(sides):
-            left = picked[0, t, s] - step0 * picked[1, t, s]
-            right = side_values(0, t, s) - step0 * side_values(1, t, s)
-            term = left * right
-            energy = term if energy is None else energy + term
-    r1 = own_buf[0] - step0 * own_buf[1]
-    r1_square = r1 * r1
-    begin_straight(lane_sums(r1_square), lane_sums(energy) + lane_sums(r1_square * diag_row))
     own_sums(1)
     wait_recv(3)
     add_returned(1)
-    new, curve = end_straight()
+    rr, curve, q_norm, q_energy = end_sum()
+    step0 = rr / curve
+    new = step0 * step0 * q_norm - rr
     beta = new / rr
-    step1 = new / (curve - beta * new / step0)
+    r1_energy = curve - 2.0 * step0 * q_norm + step0 * step0 * q_energy
+    step1 = new / (r1_energy - beta * new / step0)
     b, q, w = own_buf[0, 0:trace], own_buf[1, 0:trace], own_buf[2, 0:trace]
     r1 = b - step0 * q
     sol_ref[...] = step0 * b + step1 * (r1 + beta * b)
     res_ref[...] = r1 - step1 * (q - step0 * w + beta * q)
-    wait_near(lambda count: h_send.at[:, :, pl.ds(0, count * width)], h_send_sem)
-    sum_wait(0, (g1 - 1) + (g2 - 1) + (n - 1), s_send_sem)
+    wait_count(
+        near, near_choices, lambda count: h_send.at[pl.ds(0, 3), pl.ds(0, count)], h_send_sem.at[0]
+    )
+    wait_count(cross, cross_choices, lambda count: x_recv.at[pl.ds(0, count)], h_send_sem.at[1])
+    sum_wait(s_send_sem)
 
 
 def put_out(sol_ref, res_ref, sol_out, res_out, sems):
@@ -446,7 +505,7 @@
         dofs = sides * trace
         tiles = elements // LANES
         ghost = blocks * width
-        assert width == LANES and dofs % 16 == 8
+        assert width == LANES and dofs % 16 == 8 and trace + blocks <= pad
         cfg = (n, g1, g2, trace, sides, elements, own, blocks, width)
         dma = pltpu.SemaphoreType.DMA
         vmem = pl.BlockSpec(memory_space=pltpu.VMEM)
@@ -466,16 +525,19 @@
                 pltpu.VMEM((tiles, dofs * dofs, LANES), BF16),
                 pltpu.VMEM((WIDE, sides * elements), BF16),
                 pltpu.VMEM((WIDE, ghost), BF16),
-                pltpu.VMEM((ghost, ghost), BF16),
-                pltpu.VMEM((4, pad, ghost), F32),
-                pltpu.VMEM((4, pad, ghost), F32),
+                pltpu.VMEM((blocks, ghost, width), BF16),
+                pltpu.VMEM((ghost, sides * elements), BF16),
+                pltpu.VMEM((4, blocks, pad, width), F32),
+                pltpu.VMEM((4, blocks, pad, width), F32),
+                pltpu.VMEM((blocks * blocks, pad, width), F32),
                 pltpu.VMEM((3, pad, own), F32),
-                pltpu.VMEM((2, tiles, sides, pad, LANES), F32),
+                pltpu.VMEM((tiles, sides, pad, LANES), F32),
                 pltpu.VMEM((tiles, sides * pad, LANES), F32),
                 pltpu.VMEM((tiles, sides * pad, LANES), F32),
-                pltpu.VMEM((2, tiles, dofs + 8, LANES), F32),
-                pltpu.VMEM((g1 + g2 + n, 2, LANES), F32),
-                dma((7,)), dma(()), dma(()), dma((4,)), dma(()), dma((3,)),
+                pltpu.VMEM((tiles, dofs + 8, LANES), F32),
+                pltpu.VMEM((n, 4, LANES), F32),
+                dma((7,)), dma(()), dma((2,)), dma((4,)), dma(()), dma(()),
+                pltpu.SemaphoreType.REGULAR,
             ],
             compiler_params=pltpu.CompilerParams(
                 collective_id=0, has_side_effects=True, vmem_limit_bytes=62 * 1024 * 1024

time: 24.9 us -> 22.4 us (0.90)
  Pallas kernels: 24.2 us -> 21.6 us
    pallas_call x1, Pallas kernels: 23.5 us -> 20.9 us  [shards(): pl.pallas_call(functools.partial(kernel, cfg), out_shape=[pltpu.VMEM(rs.s...]
where the time goes in v2:
time: 22.4 us; the launch traced here: 22.2 us
  Pallas kernels  21.6 us (96%)
  between operations  0.64 us (3%)
    pallas_call x1, Pallas kernels, shards(): pl.pallas_call(functools.partial(kernel, cfg), out_shape=[pltpu.VMEM(rs.s...  20.9 us
    pallas_call x1, Pallas kernels, shards(): pl.pallas_call(put_out, out_shape=[jax.ShapeDtypeStruct(rs.shape, F32)] *...  0.69 us

profile of v2, /device:TPU:0, one launch (start us, length us, event | category | flops | bytes accessed | tf_op | source)
XLA Modules:
  0.0 22.2 jit_solution(15336918618243829010)
XLA Ops:
  0.6 20.9 %shard_map.95 = (f32[18,1024]{1,0:T(8,128)S(1)}, f32[18,1024]{1,0:T(8,128)S(1)}) custom-call(f32[18,1024]{1,0:T(8,128)} %rs_in.1, bf16[5184,512]{1,0:T(8,128)(2,1)} %bitcast.4, s32[4,512]{1,0:T(4,128)} %fm_in.1, s32[1,4,128]{2,1,0:T(4,128)} %si_in.1, s32[1,4]{1,0:T(1,128)} %sc_in.1, f32[1,1024]{1,0:T(1,128)} %bitcast.5, s32[1,1024]{1,0:T(1,128)} %bitcast.6, ...), custom_call_target="tpu_custom_call" | custom-call | tf_op jit(solution)/shard_map/pallas_call | solution.py:512
  21.6 0.7 %shard_map.96 = (f32[18,1024]{1,0:T(8,128)}, f32[18,1024]{1,0:T(8,128)}) custom-call(f32[18,1024]{1,0:T(8,128)S(1)} %get-tuple-element.4.sol_ref, f32[18,1024]{1,0:T(8,128)S(1)} %get-tuple-element.5.res_ref), custom_call_target="tpu_custom_call" | custom-call | tf_op jit(solution)/shard_map/pallas_call | solution.py:549

commit v3 on v2

--- a/solution.py
+++ b/solution.py
@@ -53,7 +53,7 @@
     own_buf, picked, x_high, x_low, prod, sums,
     in_sem, em_sem, h_send_sem, h_recv_sem, s_send_sem, s_recv_sem, ready,
 ):
-    n, g1, g2, trace, sides, elements, own, blocks, width = cfg
+    n, trace, sides, elements, own, blocks, width = cfg
     offsets = offset_list(blocks)
     pad = -(-trace // 8) * 8
     dofs = sides * trace
@@ -63,29 +63,41 @@
     own_tiles, ghost_tiles = own // LANES, ghost // LANES
     tiles = elements // LANES
     me = lax.axis_index("dom")
-    block_of, in_block = me // g1, lax.rem(me, g1)
 
     barrier = pltpu.get_barrier_semaphore()
-    waits = jnp.int32((g1 - 1) + (g2 - 1))
+    def valid(device):
+        return (device >= 0) & (device < n)
+
+    def signal(device, semaphore):
+        @pl.when(valid(device))
+        def _():
+            pl.semaphore_signal(semaphore, inc=1, device_id=(device,), device_id_type=MESH)
+
+    def count_valid(*devices):
+        return sum(valid(device).astype(jnp.int32) for device in devices)
+
     for o in offsets:
-        there = me + o
-        inside = (there >= 0) & (there < n)
-        waits = waits + inside.astype(jnp.int32)
-
-        @pl.when(inside)
-        def _():
-            pl.semaphore_signal(barrier, inc=1, device_id=(there,), device_id_type=MESH)
-
-    def peer1(d):
-        return block_of * g1 + lax.rem(in_block + d, g1)
-
-    def peer2(d):
-        return lax.rem(block_of + d, g2) * g1 + in_block
-
-    for d in range(1, g1):
-        pl.semaphore_signal(barrier, inc=1, device_id=(peer1(d),), device_id_type=MESH)
-    for d in range(1, g2):
-        pl.semaphore_signal(barrier, inc=1, device_id=(peer2(d),), device_id_type=MESH)
+        signal(me + o, barrier)
+
+    reaches = []
+    reach = 2 * max(offsets)
+    while reach < n - 1:
+        reaches.append(reach)
+        reach *= 2
+
+    def spread_word(i):
+        for device in (me - reaches[i], me + reaches[i]):
+            signal(device, ready.at[i])
+
+    def hear_word(i):
+        count = count_valid(me - reaches[i], me + reaches[i])
+        pl.semaphore_wait(ready.at[i], count)
+
+    def pass_word(i):
+        if i < len(reaches):
+            hear_word(i)
+        if i + 1 < len(reaches):
+            spread_word(i + 1)
 
     in_copies = [
         pltpu.make_async_copy(source, target, in_sem.at[i])
@@ -103,13 +115,13 @@
             em_ref.at[:, pl.ds(t * LANES, LANES)], em_buf.at[t], em_sem
         ).start()
 
-    def valid(device):
-        return (device >= 0) & (device < n)
+    def live(ref, i):
+        return ref if i == 0 else ref.at[pl.ds(0, trace)]
 
     def send_piece(source, target, device, i):
         return pltpu.make_async_remote_copy(
-            src_ref=source, dst_ref=target,
-            send_sem=h_send_sem.at[int(i == 2)], recv_sem=h_recv_sem.at[i],
+            src_ref=live(source, i), dst_ref=live(target, i),
+            send_sem=h_send_sem.at[(0, 1, 2, 1)[i]], recv_sem=h_recv_sem.at[i],
             device_id=(device,), device_id_type=MESH,
         )
 
@@ -164,9 +176,16 @@
     cross_choices = [pair[1] for pair in counts]
 
     def wait_recv(i):
+        rows = pad if i == 0 else trace
         wait_count(
-            near, near_choices, lambda count: h_recv.at[i, pl.ds(0, count)], h_recv_sem.at[i]
-        )
+            near,
+            near_choices,
+            lambda count: h_recv.at[i, pl.ds(0, count), pl.ds(0, rows)],
+            h_recv_sem.at[i],
+        )
+
+    def cross_view(count):
+        return x_recv.at[pl.ds(0, count), pl.ds(0, trace)]
 
     for copy in in_copies[:3]:
         copy.wait()
@@ -201,6 +220,13 @@
         for c in range(blocks):
             h_send[0, k, trace + c : trace + c + 1, :] = shared_index[c]
 
+    dead_rows = jnp.zeros((pad - trace, width), F32)
+    for k in range(blocks):
+        for i in (1, 3):
+            h_recv[i, k, trace:pad, :] = dead_rows
+        for c in range(blocks):
+            x_recv[k * blocks + c, trace:pad, :] = dead_rows
+
     @pl.when(cross < blocks * blocks)
     def _():
         empty = jnp.zeros((pad, width), F32)
@@ -226,10 +252,8 @@
                 def _():
                     x_recv[k * blocks + c] = empty
 
-    pl.semaphore_wait(barrier, waits)
+    pl.semaphore_wait(barrier, count_valid(*(me + o for o in offsets)))
     start_all(0)
-    for d in range(1, g1):
-        pl.semaphore_signal(ready, inc=1, device_id=(peer1(d),), device_id_type=MESH)
 
     for copy in in_copies[3:]:
         copy.wait()
@@ -337,9 +361,10 @@
             jnp.concatenate(parts, axis=1), pick_map[:, lane : lane + sides * LANES]
         )
 
-    def elements_of(rnd):
+    def elements_of(rnd, before_tile, after_products):
         ghost_total = None
         for t in range(tiles):
+            before_tile(t)
             for s in range(sides):
                 value = pick_tile(
                     lambda h: h_recv[2 * rnd, h],
@@ -350,6 +375,7 @@
                 x_high[t, s * pad : (s + 1) * pad, :] = high
                 x_low[t, s * pad : (s + 1) * pad, :] = value - high
             prod[t, 0:dofs, :] = product(t)
+        result = after_products()
         for t in range(tiles):
             part = spread(t, own_hi, ghost_hi)
             ghost_total = part if ghost_total is None else ghost_total + part
@@ -358,6 +384,7 @@
         for k in range(blocks):
             h, lane = k // per_wide, k % per_wide * width
             h_send[2 * rnd + 1, k] = ghost_total[h * pad : (h + 1) * pad, lane : lane + width]
+        return result
 
     def energy_of():
         energy = None
@@ -405,7 +432,6 @@
 
     def begin_sum(rows):
         sums[me] = jnp.concatenate(rows, axis=0)
-        pl.semaphore_wait(ready, g1 - 1)
         for d in range(n - 1):
             pltpu.make_async_remote_copy(
                 src_ref=sums.at[me], dst_ref=sums.at[me],
@@ -424,7 +450,9 @@
 
     pltpu.make_async_copy(em_buf, em_buf, em_sem).wait()
     wait_recv(0)
-    elements_of(0)
+    if reaches:
+        spread_word(0)
+    elements_of(0, lambda t: None, lambda: None)
     for copy, to in relays():
         pl.when(to)(copy.start)
     start_all(1)
@@ -433,34 +461,40 @@
         h_send[2, k] = send_values(1, k)
     for copy, to in owners():
         pl.when(to)(copy.start)
+    pass_word(0)
     b = own_buf[0]
     b_square = lane_sums(b * b)
     b_energy = energy_of() + lane_sums(b * b * diag_row)
     map_shared()
     map_returned()
     pick_own(1)
+    pass_word(1)
 
     wait_recv(1)
-    wait_count(cross, cross_choices, lambda count: x_recv.at[pl.ds(0, count)], h_recv_sem.at[2])
+    wait_count(cross, cross_choices, cross_view, h_recv_sem.at[2])
     for k in range(blocks):
         parts = jnp.concatenate(
             [h_send[1, k] if c == k else x_recv[k * blocks + c] for c in range(blocks)], axis=1
         )
         h_recv[2, k] = x_recv[k * blocks + k] + sum2(dot(split2(parts), same_map[k]))
     returned = split2(jnp.concatenate([h_recv[1, k] for k in range(blocks)], axis=1))
-    for t in range(tiles):
+
+    def take_returned(t):
         lane = t * sides * LANES
         extra = sum2(dot(returned, pick_same[:, lane : lane + sides * LANES]))
         for s in range(sides):
             picked[t, s] += extra[:, s * LANES : (s + 1) * LANES]
-    add_returned(0)
-    q = own_buf[1]
-    q_square = lane_sums(q * q)
-    q_diagonal = lane_sums(q * q * diag_row)
-
-    elements_of(1)
+
+    def finish_q():
+        add_returned(0)
+        q = own_buf[1]
+        return lane_sums(q * q), lane_sums(q * q * diag_row)
+
+    q_square, q_diagonal = elements_of(1, take_returned, finish_q)
+    start_all(3)
+    for i in range(2, len(reaches)):
+        pass_word(i)
     begin_sum([b_square, b_energy, q_square, energy_of() + q_diagonal])
-    start_all(3)
     own_sums(1)
     wait_recv(3)
     add_returned(1)
@@ -474,10 +508,14 @@
     r1 = b - step0 * q
     sol_ref[...] = step0 * b + step1 * (r1 + beta * b)
     res_ref[...] = r1 - step1 * (q - step0 * w + beta * q)
+    wait_count(near, near_choices, lambda count: h_send.at[0, pl.ds(0, count)], h_send_sem.at[0])
     wait_count(
-        near, near_choices, lambda count: h_send.at[pl.ds(0, 3), pl.ds(0, count)], h_send_sem.at[0]
+        near,
+        near_choices,
+        lambda count: h_send.at[pl.ds(1, 2), pl.ds(0, count), pl.ds(0, trace)],
+        h_send_sem.at[1],
     )
-    wait_count(cross, cross_choices, lambda count: x_recv.at[pl.ds(0, count)], h_send_sem.at[1])
+    wait_count(cross, cross_choices, cross_view, h_send_sem.at[2])
     sum_wait(s_send_sem)
 
 
@@ -494,8 +532,6 @@
 
 def solution(mesh):
     n = mesh.shape["dom"]
-    g1 = next(g for g in range(1, n + 1) if n % g == 0 and g * g >= n)
-    g2 = n // g1
 
     def shards(rs, em, fm, si, sc, mass, absorb, imp):
         trace, own = rs.shape
@@ -505,8 +541,9 @@
         dofs = sides * trace
         tiles = elements // LANES
         ghost = blocks * width
+        words = max(1, n.bit_length())
         assert width == LANES and dofs % 16 == 8 and trace + blocks <= pad
-        cfg = (n, g1, g2, trace, sides, elements, own, blocks, width)
+        cfg = (n, trace, sides, elements, own, blocks, width)
         dma = pltpu.SemaphoreType.DMA
         vmem = pl.BlockSpec(memory_space=pltpu.VMEM)
         sol, res = pl.pallas_call(
@@ -536,8 +573,8 @@
                 pltpu.VMEM((tiles, sides * pad, LANES), F32),
                 pltpu.VMEM((tiles, dofs + 8, LANES), F32),
                 pltpu.VMEM((n, 4, LANES), F32),
-                dma((7,)), dma(()), dma((2,)), dma((4,)), dma(()), dma(()),
-                pltpu.SemaphoreType.REGULAR,
+                dma((7,)), dma(()), dma((3,)), dma((4,)), dma(()), dma(()),
+                pltpu.SemaphoreType.REGULAR((words,)),
             ],
             compiler_params=pltpu.CompilerParams(
                 collective_id=0, has_side_effects=True, vmem_limit_bytes=62 * 1024 * 1024

time: 22.4 us -> 21.9 us (0.978)
  Pallas kernels: 21.6 us -> 21.1 us
    pallas_call x1, Pallas kernels: 20.9 us -> 20.4 us  [shards(): pl.pallas_call(functools.partial(kernel, cfg), out_shape=[pltpu.VMEM(rs.s...]
where the time goes in v3:
time: 21.9 us; the launch traced here: 21.7 us
  Pallas kernels  21.1 us (96%)
  between operations  0.64 us (3%)
    pallas_call x1, Pallas kernels, shards(): pl.pallas_call(functools.partial(kernel, cfg), out_shape=[pltpu.VMEM(rs.s...  20.4 us
    pallas_call x1, Pallas kernels, shards(): pl.pallas_call(put_out, out_shape=[jax.ShapeDtypeStruct(rs.shape, F32)] *...  0.69 us

profile of v3, /device:TPU:0, one launch (start us, length us, event | category | flops | bytes accessed | tf_op | source)
XLA Modules:
  0.0 21.7 jit_solution(15492879445702818490)
XLA Ops:
  0.6 20.4 %shard_map.95 = (f32[18,1024]{1,0:T(8,128)S(1)}, f32[18,1024]{1,0:T(8,128)S(1)}) custom-call(f32[18,1024]{1,0:T(8,128)} %rs_in.1, bf16[5184,512]{1,0:T(8,128)(2,1)} %bitcast.4, s32[4,512]{1,0:T(4,128)} %fm_in.1, s32[1,4,128]{2,1,0:T(4,128)} %si_in.1, s32[1,4]{1,0:T(1,128)} %sc_in.1, f32[1,1024]{1,0:T(1,128)} %bitcast.5, s32[1,1024]{1,0:T(1,128)} %bitcast.6, ...), custom_call_target="tpu_custom_call" | custom-call | tf_op jit(solution)/shard_map/pallas_call | solution.py:549
  21.0 0.7 %shard_map.96 = (f32[18,1024]{1,0:T(8,128)}, f32[18,1024]{1,0:T(8,128)}) custom-call(f32[18,1024]{1,0:T(8,128)S(1)} %get-tuple-element.4.sol_ref, f32[18,1024]{1,0:T(8,128)S(1)} %get-tuple-element.5.res_ref), custom_call_target="tpu_custom_call" | custom-call | tf_op jit(solution)/shard_map/pallas_call | solution.py:586

commit v4 on v3

--- a/solution.py
+++ b/solution.py
@@ -361,10 +361,9 @@
             jnp.concatenate(parts, axis=1), pick_map[:, lane : lane + sides * LANES]
         )
 
-    def elements_of(rnd, before_tile, after_products):
+    def elements_of(rnd):
         ghost_total = None
         for t in range(tiles):
-            before_tile(t)
             for s in range(sides):
                 value = pick_tile(
                     lambda h: h_recv[2 * rnd, h],
@@ -375,7 +374,6 @@
                 x_high[t, s * pad : (s + 1) * pad, :] = high
                 x_low[t, s * pad : (s + 1) * pad, :] = value - high
             prod[t, 0:dofs, :] = product(t)
-        result = after_products()
         for t in range(tiles):
             part = spread(t, own_hi, ghost_hi)
             ghost_total = part if ghost_total is None else ghost_total + part
@@ -384,7 +382,6 @@
         for k in range(blocks):
             h, lane = k // per_wide, k % per_wide * width
             h_send[2 * rnd + 1, k] = ghost_total[h * pad : (h + 1) * pad, lane : lane + width]
-        return result
 
     def energy_of():
         energy = None
@@ -430,6 +427,26 @@
             total = total[:, :half] + total[:, half:]
         return total
 
+    lane_of = lax.broadcasted_iota(jnp.int32, (1, LANES), 1)
+    quarter = LANES // 4
+    lane_parts = (
+        lane_of < quarter,
+        (lane_of >= quarter) & (lane_of < 2 * quarter),
+        lane_of >= 2 * quarter,
+    )
+
+    def fold(x, lanes):
+        x = jnp.broadcast_to(x, (8, LANES))
+        size = LANES // 2
+        while size >= lanes:
+            x = x + pltpu.roll(x, size, 1)
+            size //= 2
+        return x[0:1]
+
+    def one_row(x, y, z):
+        rest = jnp.where(lane_parts[1], fold(y, quarter), fold(z, 2 * quarter))
+        return jnp.where(lane_parts[0], fold(x, quarter), rest)
+
     def begin_sum(rows):
         sums[me] = jnp.concatenate(rows, axis=0)
         for d in range(n - 1):
@@ -445,17 +462,20 @@
 
     def end_sum():
         sum_wait(s_recv_sem)
-        total = jnp.sum(jnp.sum(sums[...], axis=0), axis=1, keepdims=True)
+        total = jnp.sum(sums[...], axis=0)
+        first = total[0:1]
+        rows = [jnp.where(part, first, 0.0) for part in lane_parts] + [total[1:2]]
+        total = jnp.sum(jnp.concatenate(rows, axis=0), axis=1, keepdims=True)
         return [total[i : i + 1] for i in range(4)]
 
     pltpu.make_async_copy(em_buf, em_buf, em_sem).wait()
     wait_recv(0)
     if reaches:
         spread_word(0)
-    elements_of(0, lambda t: None, lambda: None)
+    elements_of(0)
+    start_all(1)
     for copy, to in relays():
         pl.when(to)(copy.start)
-    start_all(1)
     own_sums(0)
     for k in range(blocks):
         h_send[2, k] = send_values(1, k)
@@ -471,39 +491,38 @@
     pass_word(1)
 
     wait_recv(1)
+    returned = split2(jnp.concatenate([h_recv[1, k] for k in range(blocks)], axis=1))
+    for t in range(tiles):
+        lane = t * sides * LANES
+        extra = sum2(dot(returned, pick_same[:, lane : lane + sides * LANES]))
+        for s in range(sides):
+            picked[t, s] += extra[:, s * LANES : (s + 1) * LANES]
+    add_returned(0)
+    q = own_buf[1]
+    q_square = lane_sums(q * q)
+    q_diagonal = lane_sums(q * q * diag_row)
+    early_row = one_row(b_square, b_energy, q_square)
     wait_count(cross, cross_choices, cross_view, h_recv_sem.at[2])
     for k in range(blocks):
         parts = jnp.concatenate(
             [h_send[1, k] if c == k else x_recv[k * blocks + c] for c in range(blocks)], axis=1
         )
         h_recv[2, k] = x_recv[k * blocks + k] + sum2(dot(split2(parts), same_map[k]))
-    returned = split2(jnp.concatenate([h_recv[1, k] for k in range(blocks)], axis=1))
-
-    def take_returned(t):
-        lane = t * sides * LANES
-        extra = sum2(dot(returned, pick_same[:, lane : lane + sides * LANES]))
-        for s in range(sides):
-            picked[t, s] += extra[:, s * LANES : (s + 1) * LANES]
-
-    def finish_q():
-        add_returned(0)
-        q = own_buf[1]
-        return lane_sums(q * q), lane_sums(q * q * diag_row)
-
-    q_square, q_diagonal = elements_of(1, take_returned, finish_q)
+
+    elements_of(1)
     start_all(3)
     for i in range(2, len(reaches)):
         pass_word(i)
-    begin_sum([b_square, b_energy, q_square, energy_of() + q_diagonal])
+    begin_sum([early_row, energy_of() + q_diagonal])
     own_sums(1)
     wait_recv(3)
     add_returned(1)
     rr, curve, q_norm, q_energy = end_sum()
     step0 = rr / curve
     new = step0 * step0 * q_norm - rr
-    beta = new / rr
+    beta = new * (1.0 / rr)
     r1_energy = curve - 2.0 * step0 * q_norm + step0 * step0 * q_energy
-    step1 = new / (r1_energy - beta * new / step0)
+    step1 = new / (r1_energy - beta * beta * curve)
     b, q, w = own_buf[0, 0:trace], own_buf[1, 0:trace], own_buf[2, 0:trace]
     r1 = b - step0 * q
     sol_ref[...] = step0 * b + step1 * (r1 + beta * b)
@@ -541,7 +560,7 @@
         dofs = sides * trace
         tiles = elements // LANES
         ghost = blocks * width
-        words = max(1, n.bit_length())
+        words = sum(2 * (blocks // 2) << i < n - 1 for i in range(n)) or 1
         assert width == LANES and dofs % 16 == 8 and trace + blocks <= pad
         cfg = (n, trace, sides, elements, own, blocks, width)
         dma = pltpu.SemaphoreType.DMA
@@ -572,7 +591,7 @@
                 pltpu.VMEM((tiles, sides * pad, LANES), F32),
                 pltpu.VMEM((tiles, sides * pad, LANES), F32),
                 pltpu.VMEM((tiles, dofs + 8, LANES), F32),
-                pltpu.VMEM((n, 4, LANES), F32),
+                pltpu.VMEM((n, 2, LANES), F32),
                 dma((7,)), dma(()), dma((3,)), dma((4,)), dma(()), dma(()),
                 pltpu.SemaphoreType.REGULAR((words,)),
             ],

time: 21.9 us -> 21.7 us (level)
  no operation moved by 1% of the time
where the time goes in v4:
time: 21.7 us; the launch traced here: 21.5 us
  Pallas kernels  20.9 us (96%)
  between operations  0.64 us (3%)
    pallas_call x1, Pallas kernels, shards(): pl.pallas_call(functools.partial(kernel, cfg), out_shape=[pltpu.VMEM(rs.s...  20.2 us
    pallas_call x1, Pallas kernels, shards(): pl.pallas_call(put_out, out_shape=[jax.ShapeDtypeStruct(rs.shape, F32)] *...  0.69 us

profile of v4, /device:TPU:0, one launch (start us, length us, event | category | flops | bytes accessed | tf_op | source)
XLA Modules:
  0.0 21.5 jit_solution(13478332826374239664)
XLA Ops:
  0.6 20.2 %shard_map.95 = (f32[18,1024]{1,0:T(8,128)S(1)}, f32[18,1024]{1,0:T(8,128)S(1)}) custom-call(f32[18,1024]{1,0:T(8,128)} %rs_in.1, bf16[5184,512]{1,0:T(8,128)(2,1)} %bitcast.4, s32[4,512]{1,0:T(4,128)} %fm_in.1, s32[1,4,128]{2,1,0:T(4,128)} %si_in.1, s32[1,4]{1,0:T(1,128)} %sc_in.1, f32[1,1024]{1,0:T(1,128)} %bitcast.5, s32[1,1024]{1,0:T(1,128)} %bitcast.6, ...), custom_call_target="tpu_custom_call" | custom-call | tf_op jit(solution)/shard_map/pallas_call | solution.py:568
  20.8 0.7 %shard_map.96 = (f32[18,1024]{1,0:T(8,128)}, f32[18,1024]{1,0:T(8,128)}) custom-call(f32[18,1024]{1,0:T(8,128)S(1)} %get-tuple-element.4.sol_ref, f32[18,1024]{1,0:T(8,128)S(1)} %get-tuple-element.5.res_ref), custom_call_target="tpu_custom_call" | custom-call | tf_op jit(solution)/shard_map/pallas_call | solution.py:605

commit v5 on v4

--- a/solution.py
+++ b/solution.py
@@ -510,10 +510,10 @@
         h_recv[2, k] = x_recv[k * blocks + k] + sum2(dot(split2(parts), same_map[k]))
 
     elements_of(1)
-    start_all(3)
     for i in range(2, len(reaches)):
         pass_word(i)
     begin_sum([early_row, energy_of() + q_diagonal])
+    start_all(3)
     own_sums(1)
     wait_recv(3)
     add_returned(1)

time: 21.7 us -> 21.6 us (level)
  no operation moved by 1% of the time
where the time goes in v5:
time: 21.6 us; the launch traced here: 21.5 us
  Pallas kernels  20.8 us (96%)
  between operations  0.64 us (3%)
    pallas_call x1, Pallas kernels, shards(): pl.pallas_call(functools.partial(kernel, cfg), out_shape=[pltpu.VMEM(rs.s...  20.1 us
    pallas_call x1, Pallas kernels, shards(): pl.pallas_call(put_out, out_shape=[jax.ShapeDtypeStruct(rs.shape, F32)] *...  0.69 us

profile of v5, /device:TPU:0, one launch (start us, length us, event | category | flops | bytes accessed | tf_op | source)
XLA Modules:
  0.0 21.5 jit_solution(17625135296319548094)
XLA Ops:
  0.6 20.1 %shard_map.95 = (f32[18,1024]{1,0:T(8,128)S(1)}, f32[18,1024]{1,0:T(8,128)S(1)}) custom-call(f32[18,1024]{1,0:T(8,128)} %rs_in.1, bf16[5184,512]{1,0:T(8,128)(2,1)} %bitcast.4, s32[4,512]{1,0:T(4,128)} %fm_in.1, s32[1,4,128]{2,1,0:T(4,128)} %si_in.1, s32[1,4]{1,0:T(1,128)} %sc_in.1, f32[1,1024]{1,0:T(1,128)} %bitcast.5, s32[1,1024]{1,0:T(1,128)} %bitcast.6, ...), custom_call_target="tpu_custom_call" | custom-call | tf_op jit(solution)/shard_map/pallas_call | solution.py:568
  20.8 0.7 %shard_map.96 = (f32[18,1024]{1,0:T(8,128)}, f32[18,1024]{1,0:T(8,128)}) custom-call(f32[18,1024]{1,0:T(8,128)S(1)} %get-tuple-element.4.sol_ref, f32[18,1024]{1,0:T(8,128)S(1)} %get-tuple-element.5.res_ref), custom_call_target="tpu_custom_call" | custom-call | tf_op jit(solution)/shard_map/pallas_call | solution.py:605
